TPU v7x, 32 devices: a whole 2x2x4 slice. The times are simulated.
32 devices in a mesh: dp: 1, expert: 32 (over z, y, x, core).
Axes of the slice: x: 2, y: 2, z: 4, core: 2. Of those that a mesh axis runs over, the one named last changes fastest.
Arguments:
- tokens: bfloat16 [4096, 1024], P(('dp', 'expert')), may hold values from -6 to 6
- cotangent: bfloat16 [4096, 1024], P(('dp', 'expert')), may hold values from -0.1875 to 0.1875
- expert_ids: int32 [4096, 4], P(('dp', 'expert')), may hold values from 0 to 31, all different within a row; in each aligned block of 128 rows (0 to 127, 128 to 255, ...) at most 32 rows name the same one
- gate_probs: bfloat16 [4096, 4], P(('dp', 'expert')), may hold values from 0.019897461 to 0.59765625
- home_share: int32 [16], replicated, may hold values from 8 to 16
- gate_weight: bfloat16 [32, 1024, 384], P('expert'), may hold values from -0.1875 to 0.1875
- up_weight: bfloat16 [32, 1024, 384], P('expert'), may hold values from -0.1875 to 0.1875
- down_weight: bfloat16 [32, 384, 1024], P('expert'), may hold values from -0.3125 to 0.3125
Outputs:
- gate_cotangent: float32 [4096, 4], P(('dp', 'expert'))
- grad_gate: float32 [32, 1024, 384], P('expert', 'dp')
- grad_up: float32 [32, 1024, 384], P('expert', 'dp')
- grad_down: float32 [32, 384, 1024], P('expert', 'dp')
Inputs may be any that keep to these rules, and one draw needn't show every extreme that they name: `expert_ids`: each token names 4 different experts; among the tokens of one device no expert is named more than 32 times.
All inputs are finite; a program needn't handle non-finite values.
Results may differ from a plain program's by a relative error of at most 0.017.
Values may be sent and summed in bfloat16 or wider, within the bound.
No kernel may reach another device: no remote copies, remote signals or barrier semaphores. Data moves between devices by JAX's collectives and lax.ppermute only.
A program may use at most 64 MiB of HBM per device.

v0:
```python
import jax
import jax.numpy as jnp
from jax import lax
from jax.sharding import PartitionSpec as P


def from_behind(block, axis, distance):
    devices = range(lax.axis_size(axis))
    route = [(i - distance, i) for i in devices if i - distance in devices]
    return lax.ppermute(block, axis, route)


def shortened(value):

    def short(part):
        return part.astype(jnp.bfloat16) if part.dtype == jnp.float32 else part

    return jax.tree.map(short, value)


def route_rows(expert_ids, home_share, experts, cap_own, cap_rep):
    half_axis = experts // 2
    capacity = cap_own + cap_rep
    flat_ids = expert_ids.reshape(-1)
    columns = jnp.arange(experts, dtype=jnp.int32)
    onehot = (flat_ids[:, None] == columns[None, :]).astype(jnp.int32)
    before = jnp.cumsum(onehot, axis=0) - onehot
    row_rank = jnp.sum(before * onehot, axis=1)
    limits = jnp.concatenate([home_share, jnp.full((experts - half_axis,), cap_own, jnp.int32)])
    home_limit = jnp.sum(onehot * limits[None, :], axis=1)
    at_home = row_rank < home_limit
    overflow = row_rank - home_limit
    to_copy = (flat_ids < half_axis) & (overflow >= 0) & (overflow < cap_rep)
    target = jnp.where(to_copy, flat_ids + half_axis, flat_ids)
    slot_index = jnp.where(to_copy, cap_own + overflow, row_rank)
    position = jnp.where(at_home | to_copy, target * capacity + slot_index, experts * capacity)
    return position.reshape(expert_ids.shape)


def expert_side(inputs, grads_out, weights_row, gate_weight, up_weight, down_weight):
    hidden_units = gate_weight.shape[1]
    gate_act = jnp.dot(inputs, gate_weight, preferred_element_type=jnp.float32)
    up_act = jnp.dot(inputs, up_weight, preferred_element_type=jnp.float32)
    sigmoid_gate = jax.nn.sigmoid(gate_act)
    silu_gate = gate_act * sigmoid_gate
    hidden = (silu_gate * up_act).astype(jnp.bfloat16)
    output = jnp.dot(hidden, down_weight, preferred_element_type=jnp.float32)
    upstream = grads_out.astype(jnp.float32)
    gate_cot = jnp.sum(upstream * output, axis=1)
    scaled = (weights_row.astype(jnp.float32)[:, None] * upstream).astype(jnp.bfloat16)
    hidden_cot = lax.dot_general(
        scaled, down_weight, (((1,), (1,)), ((), ())), preferred_element_type=jnp.float32
    )
    gate_pre = (
        hidden_cot * up_act * sigmoid_gate * (1.0 + gate_act * (1.0 - sigmoid_gate))
    ).astype(jnp.bfloat16)
    up_pre = (hidden_cot * silu_gate).astype(jnp.bfloat16)
    both_pre = jnp.concatenate([gate_pre, up_pre], axis=1)
    both_grad = lax.dot_general(
        inputs, both_pre, (((0,), (0,)), ((), ())), preferred_element_type=jnp.float32
    ).astype(jnp.bfloat16)
    grad_down = lax.dot_general(
        hidden, scaled, (((0,), (0,)), ((), ())), preferred_element_type=jnp.float32
    ).astype(jnp.bfloat16)
    return (gate_cot, both_grad[:, :hidden_units], both_grad[:, hidden_units:], grad_down)


def per_device(
    tokens, cotangent, expert_ids, gate_probs, home_share, gate_weight, up_weight, down_weight
):
    experts = lax.axis_size("expert")
    tok_rows, model_width = tokens.shape
    top_count = expert_ids.shape[1]
    cap_own = tok_rows * top_count // experts
    cap_rep = cap_own // 4
    capacity = cap_own + cap_rep
    half_axis = experts // 2
    slots_total = experts * capacity
    position = route_rows(expert_ids, home_share, experts, cap_own, cap_rep)
    spread = position.shape + (model_width,)
    row_buffer = jnp.zeros((slots_total + 1, model_width), jnp.bfloat16)
    row_buffer = row_buffer.at[position].set(jnp.broadcast_to(tokens[:, None, :], spread))
    cot_buffer = jnp.zeros((slots_total + 1, model_width), jnp.bfloat16)
    cot_buffer = cot_buffer.at[position].set(jnp.broadcast_to(cotangent[:, None, :], spread))
    prob_buffer = jnp.zeros((slots_total + 1,), jnp.bfloat16).at[position].set(gate_probs)
    send_rows = row_buffer[:-1].reshape(experts, capacity, model_width)
    send_cots = cot_buffer[:-1].reshape(experts, capacity, model_width)
    send_probs = prob_buffer[:-1].reshape(experts, capacity)
    recv_rows, recv_probs = (
        lax.all_to_all(send_rows, "expert", split_axis=0, concat_axis=0, tiled=True),
        lax.all_to_all(send_probs, "expert", split_axis=0, concat_axis=0, tiled=True),
    )
    recv_cots = lax.all_to_all(send_cots, "expert", split_axis=0, concat_axis=0, tiled=True)
    home_weights = (gate_weight[0], up_weight[0], down_weight[0])
    copies = from_behind((home_weights[0], home_weights[1], home_weights[2]), "expert", half_axis)
    own_out = expert_side(
        recv_rows[:, :cap_own].reshape(-1, model_width),
        recv_cots[:, :cap_own].reshape(-1, model_width),
        recv_probs[:, :cap_own].reshape(-1),
        home_weights[0],
        home_weights[1],
        home_weights[2],
    )
    rep_out = expert_side(
        recv_rows[:, cap_own:].reshape(-1, model_width),
        recv_cots[:, cap_own:].reshape(-1, model_width),
        recv_probs[:, cap_own:].reshape(-1),
        copies[0],
        copies[1],
        copies[2],
    )
    gate_cot = jnp.concatenate(
        [own_out[0].reshape(experts, cap_own), rep_out[0].reshape(experts, cap_rep)], axis=1
    )
    returned = lax.all_to_all(gate_cot, "expert", split_axis=0, concat_axis=0, tiled=True)
    gate_grads = jnp.concatenate([returned.reshape(-1), jnp.zeros((1,), jnp.float32)])[position]
    own_bf = own_out[1:]
    copy_bf = rep_out[1:]
    sent_home = jax.tree.map(
        lambda part, own: part.astype(own.dtype),
        from_behind(shortened(copy_bf), "expert", -half_axis),
        copy_bf,
    )
    device_terms = tuple(
        (
            local_part.astype(jnp.float32) + remote_part.astype(jnp.float32)
            for local_part, remote_part in zip(own_bf, sent_home)
        )
    )
    summed = jax.tree.map(
        lambda part: part.astype(jnp.float32),
        lax.psum_scatter(shortened(device_terms), "dp", scatter_dimension=0, tiled=True),
    )
    return (gate_grads, summed[0][None], summed[1][None], summed[2][None])


def solution(mesh):
    return jax.shard_map(
        per_device,
        mesh=mesh,
        in_specs=(
            P(("dp", "expert"), None),
            P(("dp", "expert"), None),
            P(("dp", "expert"), None),
            P(("dp", "expert"), None),
            P(),
            P("expert", None, None),
            P("expert", None, None),
            P("expert", None, None),
        ),
        out_specs=(
            P(("dp", "expert"), None),
            P("expert", "dp", None),
            P("expert", "dp", None),
            P("expert", "dp", None),
        ),
        check_vma=False,
    )
```

profile of v0, /device:TPU:0, one launch (start us, length us, event | category | flops | bytes accessed | tf_op | source)
XLA Modules:
  0.0 307.7 jit_solution(2535125659640893300)
XLA Ops:
  0.6 0.7 broadcast_compare_fusion
  1.3 0.7 broadcast_add_fusion
  2.0 0.8 copy.34
  3.0 0.1 copy.38
  3.1 0.8 copy.43
  4.0 0.1 reshape.131
  4.2 1.2 reduce-window.6
  5.4 0.2 slice_reduce_fusion
  5.6 0.7 concatenate.15
  6.8 3.8 %scatter_custom_fusion.2 = bf16[641]{0:T(1024)(128)(2,1)S(1)} fusion(s32[512]{0:T(512)S(1)} %reshape.113, bf16[512]{0:T(512)(128)(2,1)S(1)} %reshape.131, bf16[]{:T(256)} %constant.10.clone.1), kind=kCustom, calls=%fused_computation.65 | custom fusion | bytes 1284 | tf_op jit(solution)/shard_map/scatter | solution.py:85
  10.6 0.7 all_to_all.27
  11.3 7.3 %all-to-all-start.3 = ((bf16[32,1,20]{2,1,0:T(2,128)(2,1)}), bf16[32,1,20]{2,1,0:T(2,128)(2,1)S(1)}, u32[]{:S(2)}, u32[]{:S(2)}) async-start(bf16[32,1,20]{2,1,0:T(2,128)(2,1)} %all_to_all.27), calls=%async_computation.3 | async-start | bytes 32768 | tf_op jit(solution)/shard_map/all_to_all | solution.py:91
  18.6 1.3 broadcast_in_dim.50
  19.9 0.3 reshape.123
  20.2 2.9 scatter_custom_fusion.1
  23.2 1.3 reshape.90
  24.5 1.2 all-to-all-done.3
  25.7 4.6 %all-to-all-start.1 = ((bf16[32,20,1024]{2,1,0:T(8,128)(2,1)}), bf16[32,20,1024]{2,1,0:T(8,128)(2,1)S(1)}, u32[]{:S(2)}, u32[]{:S(2)}) async-start(bf16[32,20,1024]{2,1,0:T(8,128)(2,1)} %reshape.90), calls=%async_computation.1 | async-start | bytes 3145728 | tf_op jit(solution)/shard_map/all_to_all | solution.py:90
  30.4 0.3 broadcast_in_dim.49
  30.7 1.1 reshape.115
  31.8 3.6 %scatter_custom_fusion = bf16[641,1024]{1,0:T(8,128)(2,1)S(1)} fusion(s32[512]{0:T(512)S(1)} %reshape.113, bf16[512,1024]{1,0:T(8,128)(2,1)} %reshape.115, bf16[]{:T(256)} %constant.10.clone.1), kind=kCustom, calls=%fused_computation.35 | custom fusion | bytes 1313280 | tf_op jit(solution)/shard_map/scatter | solution.py:84
  35.4 1.2 slice.63
  36.5 3.2 %reshape.89 = bf16[32,20,1024]{2,1,0:T(8,128)(2,1)} reshape(bf16[640,1024]{1,0:T(8,128)(2,1)} %slice.63) | data formatting | bytes 2621440 | tf_op jit(solution)/shard_map/reshape | solution.py:87
  39.7 28.3 %all-to-all-done.1 = bf16[32,20,1024]{2,1,0:T(8,128)(2,1)S(1)} async-done(((bf16[32,20,1024]{2,1,0:T(8,128)(2,1)}), bf16[32,20,1024]{2,1,0:T(8,128)(2,1)S(1)}, u32[]{:S(2)}, u32[]{:S(2)}) %all-to-all-start.1) | async-done | bytes 1310752 | tf_op jit(solution)/shard_map/all_to_all | solution.py:90
  68.0 3.8 %all-to-all-start = ((bf16[32,20,1024]{2,1,0:T(8,128)(2,1)}), bf16[32,20,1024]{2,1,0:T(8,128)(2,1)S(1)}, u32[]{:S(2)}, u32[]{:S(2)}) async-start(bf16[32,20,1024]{2,1,0:T(8,128)(2,1)} %reshape.89), calls=%async_computation | async-start | bytes 3145728 | tf_op jit(solution)/shard_map/all_to_all | solution.py:93
  71.8 5.5 %collective-permute-start.2 = (bf16[384,1024]{1,0:T(8,128)(2,1)}, bf16[384,1024]{1,0:T(8,128)(2,1)}, u32[]{:S(2)}, u32[]{:S(2)}) collective-permute-start(bf16[384,1024]{1,0:T(8,128)(2,1)} %bitcast.85), channel_id=1, source_target_pairs={{0,16},{1,17},{2,18},{3,19},{4,20},{5,21},{6,22},{7,23},{8,24},{9,... | collective-permute-start | bytes 2359304 | tf_op jit(solution)/shard_map/ppermute | solution.py:10
  77.3 2.2 collective-permute-start.1
  79.5 2.4 collective-permute-start
  82.5 27.0 %all-to-all-done = bf16[32,20,1024]{2,1,0:T(8,128)(2,1)S(1)} async-done(((bf16[32,20,1024]{2,1,0:T(8,128)(2,1)}), bf16[32,20,1024]{2,1,0:T(8,128)(2,1)S(1)}, u32[]{:S(2)}, u32[]{:S(2)}) %all-to-all-start) | async-done | bytes 1310752 | tf_op jit(solution)/shard_map/all_to_all | solution.py:93
  109.6 0.2 reshape.97
  109.8 1.3 slice.66
  111.1 21.2 %collective-permute-done.1 = bf16[1024,384]{1,0:T(8,128)(2,1)} collective-permute-done((bf16[1024,384]{1,0:T(8,128)(2,1)}, bf16[1024,384]{1,0:T(8,128)(2,1)}, u32[]{:S(2)}, u32[]{:S(2)}) %collective-permute-start.1) | collective-permute-done | bytes 786464 | tf_op jit(solution)/shard_map/ppermute | solution.py:10
  132.3 1.4 fusion.39
  133.8 1.5 fusion.37
  135.3 1.5 fusion.33
  136.8 12.0 %collective-permute-done = bf16[1024,384]{1,0:T(8,128)(2,1)} collective-permute-done((bf16[1024,384]{1,0:T(8,128)(2,1)}, bf16[1024,384]{1,0:T(8,128)(2,1)}, u32[]{:S(2)}, u32[]{:S(2)}) %collective-permute-start) | collective-permute-done | bytes 786464 | tf_op jit(solution)/shard_map/ppermute | solution.py:10
  148.8 2.2 multiply_convert_fusion.5
  151.0 1.3 convolution_convert_fusion.2
  152.3 1.5 fusion.5
  154.0 1.4 collective-permute-start.5
  155.4 0.2 fusion
  155.7 0.6 fusion.30
  156.3 0.5 copy-done.4
  156.8 0.2 copy-done.9
  157.0 1.9 multiply_convert_fusion.1
  159.0 0.7 copy-done.5
  159.6 0.8 fusion.1
  160.5 0.7 pad_maximum_fusion
  161.2 66.7 %all-to-all-start.2 = ((f32[32,1,20]{2,1,0:T(1,128)}), f32[32,1,20]{2,1,0:T(1,128)S(1)}, u32[]{:S(2)}, u32[]{:S(2)}) async-start(f32[32,1,20]{2,1,0:T(1,128)} %bitcast.7), calls=%async_computation.2 | async-start | bytes 32768 | tf_op jit(solution)/shard_map/all_to_all | solution.py:115
  227.9 0.6 convolution_convert_fusion.1
  228.5 1.3 fusion.38
  229.9 1.3 collective-permute-start.4
  231.1 1.3 collective-permute-start.3
  232.5 2.2 convolution_convert_fusion
  234.6 0.2 fusion.2
  234.9 37.8 %all-to-all-done.2 = f32[32,1,20]{2,1,0:T(1,128)S(1)} async-done(((f32[32,1,20]{2,1,0:T(1,128)}), f32[32,1,20]{2,1,0:T(1,128)S(1)}, u32[]{:S(2)}, u32[]{:S(2)}) %all-to-all-start.2) | async-done | bytes 2592 | tf_op jit(solution)/shard_map/all_to_all | solution.py:115
  272.7 0.5 broadcast.82
  273.2 0.7 reduce.5
  274.0 2.3 gather_fusion
  276.4 0.7 copy.49
  277.1 3.0 fusion.4
  280.1 7.6 %collective-permute-done.4 = bf16[1024,384]{1,0:T(8,128)(2,1)S(1)} collective-permute-done((bf16[1024,384]{1,0:T(8,128)(2,1)}, bf16[1024,384]{1,0:T(8,128)(2,1)S(1)}, u32[]{:S(2)}, u32[]{:S(2)}) %collective-permute-start.4) | collective-permute-done | bytes 786464 | tf_op jit(solution)/shard_map/ppermute | solution.py:10
  287.7 16.9 %collective-permute-done.3 = bf16[1024,384]{1,0:T(8,128)(2,1)} collective-permute-done((bf16[1024,384]{1,0:T(8,128)(2,1)}, bf16[1024,384]{1,0:T(8,128)(2,1)}, u32[]{:S(2)}, u32[]{:S(2)}) %collective-permute-start.3) | collective-permute-done | bytes 786464 | tf_op jit(solution)/shard_map/ppermute | solution.py:10
  304.6 3.1 %fusion.9 = (f32[1,1024,384]{2,1,0:T(8,128)}, f32[1,1024,384]{2,1,0:T(8,128)}) fusion(bf16[1024,384]{1,0:T(8,128)(2,1)S(1)} %collective-permute-done.4, bf16[1024,768]{1,0:T(8,128)(2,1)S(1)} %copy-done.1, bf16[1024,384]{1,0:T(8,128)(2,1)} %collective-permute-done.3), kind=kLoop, calls=%fused_computation.24 | loop fusion | flops 3932160 | bytes 6291456 | tf_op jit(solution)/shard_map/broadcast_in_dim | solution.py:134
  (52 shorter events, 2.2 us)
Async XLA Ops:
  11.3 14.4 %all-to-all-start.3 = ((bf16[32,1,20]{2,1,0:T(2,128)(2,1)}), bf16[32,1,20]{2,1,0:T(2,128)(2,1)S(1)}, u32[]{:S(2)}, u32[]{:S(2)}) async-start(bf16[32,1,20]{2,1,0:T(2,128)(2,1)} %all_to_all.27), calls=%async_computation.3 | async-start | bytes 32768 | tf_op jit(solution)/shard_map/all_to_all | solution.py:91
  24.5 5.8 %copy-start.7 = (bf16[128,1024]{1,0:T(8,128)(2,1)S(1)}, bf16[128,1024]{1,0:T(8,128)(2,1)}, u32[]{:S(2)}) copy-start(bf16[128,1024]{1,0:T(8,128)(2,1)} %param.9) | copy-start | bytes 786436
  25.7 42.2 %all-to-all-start.1 = ((bf16[32,20,1024]{2,1,0:T(8,128)(2,1)}), bf16[32,20,1024]{2,1,0:T(8,128)(2,1)S(1)}, u32[]{:S(2)}, u32[]{:S(2)}) async-start(bf16[32,20,1024]{2,1,0:T(8,128)(2,1)} %reshape.90), calls=%async_computation.1 | async-start | bytes 3145728 | tf_op jit(solution)/shard_map/all_to_all | solution.py:90
  68.0 14.3 %copy-start = (bf16[32,20,1024]{2,1,0:T(8,128)(2,1)}, bf16[32,20,1024]{2,1,0:T(8,128)(2,1)S(1)}, u32[]{:S(2)}) copy-start(bf16[32,20,1024]{2,1,0:T(8,128)(2,1)S(1)} %all-to-all-done.1) | copy-start | bytes 3932164
  68.0 41.5 %all-to-all-start = ((bf16[32,20,1024]{2,1,0:T(8,128)(2,1)}), bf16[32,20,1024]{2,1,0:T(8,128)(2,1)S(1)}, u32[]{:S(2)}, u32[]{:S(2)}) async-start(bf16[32,20,1024]{2,1,0:T(8,128)(2,1)} %reshape.89), calls=%async_computation | async-start | bytes 3145728 | tf_op jit(solution)/shard_map/all_to_all | solution.py:93
  71.8 61.9 %collective-permute-start.2 = (bf16[384,1024]{1,0:T(8,128)(2,1)}, bf16[384,1024]{1,0:T(8,128)(2,1)}, u32[]{:S(2)}, u32[]{:S(2)}) collective-permute-start(bf16[384,1024]{1,0:T(8,128)(2,1)} %bitcast.85), channel_id=1, source_target_pairs={{0,16},{1,17},{2,18},{3,19},{4,20},{5,21},{6,22},{7,23},{8,24},{9,... | collective-permute-start | bytes 2359304 | tf_op jit(solution)/shard_map/ppermute | solution.py:10
  77.3 55.0 %collective-permute-start.1 = (bf16[1024,384]{1,0:T(8,128)(2,1)}, bf16[1024,384]{1,0:T(8,128)(2,1)}, u32[]{:S(2)}, u32[]{:S(2)}) collective-permute-start(bf16[1024,384]{1,0:T(8,128)(2,1)} %bitcast.84), channel_id=1, source_target_pairs={{0,16},{1,17},{2,18},{3,19},{4,20},{5,21},{6,22},{7,23},{8,24},{9,... | collective-permute-start | bytes 2359304 | tf_op jit(solution)/shard_map/ppermute | solution.py:10
  79.5 69.4 %collective-permute-start = (bf16[1024,384]{1,0:T(8,128)(2,1)}, bf16[1024,384]{1,0:T(8,128)(2,1)}, u32[]{:S(2)}, u32[]{:S(2)}) collective-permute-start(bf16[1024,384]{1,0:T(8,128)(2,1)} %bitcast.89), channel_id=1, source_target_pairs={{0,16},{1,17},{2,18},{3,19},{4,20},{5,21},{6,22},{7,23},{8,24},{9,... | collective-permute-start | bytes 2359304 | tf_op jit(solution)/shard_map/ppermute | solution.py:10
  111.1 24.2 %copy-start.2 = (bf16[1,1024,384]{2,1,0:T(8,128)(2,1)S(1)}, bf16[1,1024,384]{2,1,0:T(8,128)(2,1)}, u32[]{:S(2)}) copy-start(bf16[1,1024,384]{2,1,0:T(8,128)(2,1)} %param.14) | copy-start | bytes 2359300
  153.9 1.7 copy-start.3
  154.0 123.1 %collective-permute-start.5 = (bf16[384,1024]{1,0:T(8,128)(2,1)}, bf16[384,1024]{1,0:T(8,128)(2,1)}, u32[]{:S(2)}, u32[]{:S(2)}) collective-permute-start(bf16[384,1024]{1,0:T(8,128)(2,1)} %convolution_convert_fusion.2), channel_id=1, source_target_pairs={{16,0},{17,1},{18,2},{19,3},{20,4},{21,5},{22,6},{23,7},{24,8},{25... | collective-permute-start | bytes 2359304 | tf_op jit(solution)/shard_map/ppermute | solution.py:10
  155.6 1.1 copy-start.4
  155.6 1.4 copy-start.9
  158.9 0.8 copy-start.5
  159.6 68.3 %copy-start.8 = (bf16[128,384]{1,0:T(8,128)(2,1)S(1)}, bf16[128,384]{1,0:T(8,128)(2,1)}, u32[]{:S(2)}) copy-start(bf16[128,384]{1,0:T(8,128)(2,1)} %get-tuple-element.26) | copy-start | bytes 294916
  161.2 111.5 %all-to-all-start.2 = ((f32[32,1,20]{2,1,0:T(1,128)}), f32[32,1,20]{2,1,0:T(1,128)S(1)}, u32[]{:S(2)}, u32[]{:S(2)}) async-start(f32[32,1,20]{2,1,0:T(1,128)} %bitcast.7), calls=%async_computation.2 | async-start | bytes 32768 | tf_op jit(solution)/shard_map/all_to_all | solution.py:115
  228.5 3.9 %copy-start.10 = (bf16[512,384]{0,1:T(8,128)(2,1)S(1)}, bf16[512,384]{0,1:T(8,128)(2,1)}, u32[]{:S(2)}) copy-start(bf16[512,384]{0,1:T(8,128)(2,1)} %get-tuple-element.22) | copy-start | bytes 1179652
  228.5 3.9 %copy-start.11 = (bf16[512,384]{0,1:T(8,128)(2,1)S(1)}, bf16[512,384]{0,1:T(8,128)(2,1)}, u32[]{:S(2)}) copy-start(bf16[512,384]{0,1:T(8,128)(2,1)} %get-tuple-element.23) | copy-start | bytes 1179652
  229.9 57.8 %collective-permute-start.4 = (bf16[1024,384]{1,0:T(8,128)(2,1)}, bf16[1024,384]{1,0:T(8,128)(2,1)S(1)}, u32[]{:S(2)}, u32[]{:S(2)}) collective-permute-start(bf16[1024,384]{1,0:T(8,128)(2,1)} %get-tuple-element.20), channel_id=1, source_target_pairs={{16,0},{17,1},{18,2},{19,3},{20,4},{21,5},{22,6},{23,7},{24,8},{25... | collective-permute-start | bytes 2359304 | tf_op jit(solution)/shard_map/ppermute | solution.py:10
  231.1 73.4 %collective-permute-start.3 = (bf16[1024,384]{1,0:T(8,128)(2,1)}, bf16[1024,384]{1,0:T(8,128)(2,1)}, u32[]{:S(2)}, u32[]{:S(2)}) collective-permute-start(bf16[1024,384]{1,0:T(8,128)(2,1)} %get-tuple-element.21), channel_id=1, source_target_pairs={{16,0},{17,1},{18,2},{19,3},{20,4},{21,5},{22,6},{23,7},{24,8},{25... | collective-permute-start | bytes 2359304 | tf_op jit(solution)/shard_map/ppermute | solution.py:10
  274.0 3.1 %copy-start.6 = (bf16[512,384]{0,1:T(8,128)(2,1)S(1)}, bf16[512,384]{0,1:T(8,128)(2,1)}, u32[]{:S(2)}) copy-start(bf16[512,384]{0,1:T(8,128)(2,1)} %copy-done.5) | copy-start | bytes 1179652
  277.1 27.5 %copy-start.1 = (bf16[1024,768]{1,0:T(8,128)(2,1)S(1)}, bf16[1024,768]{1,0:T(8,128)(2,1)}, u32[]{:S(2)}) copy-start(bf16[1024,768]{1,0:T(8,128)(2,1)} %convolution_convert_fusion) | copy-start | bytes 4718596
where the time goes:
time: 309 us; the launch traced here: 308 us
  waiting for transfers between devices  152 us (49%)
  starting transfers between devices  96.4 us (31%)
  local copies, waits for them, and re-layouts  31.8 us (10%)
  matrix products  18.5 us (6%)
  other arithmetic  7.84 us (3%)
    all_to_all x1, starting transfers between devices, per_device(): lax.all_to_all(gate_cot, 'expert', split_axis=0, concat_axis=0, tiled=True)  66.7 us
    ppermute x6, waiting for transfers between devices, from_behind(): return lax.ppermute(block, axis, route)  57.7 us
    all_to_all x1, waiting for transfers between devices, per_device(): lax.all_to_all(gate_cot, 'expert', split_axis=0, concat_axis=0, tiled=True)  37.8 us
    all_to_all x1, waiting for transfers between devices, per_device(): lax.all_to_all(send_rows, 'expert', split_axis=0, concat_axis=0, tiled=True)  28.3 us
    all_to_all x1, waiting for transfers between devices, per_device(): lax.all_to_all(send_cots, 'expert', split_axis=0, concat_axis=0, tiled=True)  27 us
    ppermute x6, starting transfers between devices, from_behind(): return lax.ppermute(block, axis, route)  14 us
    all_to_all x1, starting transfers between devices, per_device(): lax.all_to_all(send_probs, 'expert', split_axis=0, concat_axis=0, tiled=T...  7.33 us
  transfers between devices with their start and end apart: 10, of which 8 were waited for; matrix products, arithmetic and copies ran while one was open for 12% of the time, Pallas kernels for 0%

commit v1 on v0

v1 whole, which is shorter than its diff:
```python
import functools
import jax
import jax.numpy as jnp
from jax import lax
from jax.experimental import pallas as pl
from jax.experimental.pallas import tpu as pltpu
from jax.sharding import PartitionSpec as P

BF16 = jnp.bfloat16
F32 = jnp.float32
VMEM = pl.BlockSpec(memory_space=pltpu.VMEM)
SMEM = pl.BlockSpec(memory_space=pltpu.SMEM)


def slot_plan(cap):
    main = cap // 8 * 8
    rest = cap - main
    return main, rest, 2 * main + -(-2 * rest // 8) * 8


def ranks(ids, share_ref, base, count, half, cap_own, cap_rep):
    tokens = ids.shape[1]
    expert = base + lax.broadcasted_iota(jnp.int32, (count, tokens), 0)
    named = jnp.zeros((count, tokens), F32)
    for choice in range(ids.shape[0]):
        named = named + jnp.where(ids[choice : choice + 1, :] == expert, 1.0, 0.0)
    earlier = lax.broadcasted_iota(jnp.int32, (tokens, tokens), 0) < lax.broadcasted_iota(
        jnp.int32, (tokens, tokens), 1
    )
    rank = jnp.dot(
        named.astype(BF16), jnp.where(earlier, 1.0, 0.0).astype(BF16), preferred_element_type=F32
    )
    limit = jnp.full((count, tokens), cap_own, jnp.int32)
    for index in range(half):
        limit = jnp.where(expert == index, share_ref[index] + cap_rep, limit)
    kept = (named > 0.5) & (rank < limit.astype(F32))
    return expert, jnp.where(kept, rank, -1.0)


def pack_rows(ids, probs, data, share_ref, base, count, half, cap_own, cap_rep):
    main, rest, chunk = slot_plan(cap_own + cap_rep)
    tokens = ids.shape[1]
    expert, rank = ranks(ids, share_ref, base, count, half, cap_own, cap_rep)
    weight = jnp.zeros((count, tokens), F32)
    for choice in range(ids.shape[0]):
        weight = weight + jnp.where(ids[choice : choice + 1, :] == expert, probs[choice : choice + 1, :], 0.0)
    line = lax.broadcasted_iota(jnp.int32, (chunk, tokens), 0)
    tail = line - 2 * main
    row_slot = jnp.where(line < main, line, jnp.where((tail >= 0) & (tail < rest), main + tail, -2))
    cot_slot = jnp.where(
        (line >= main) & (line < 2 * main),
        line - main,
        jnp.where((tail >= rest) & (tail < 2 * rest), main + tail - rest, -2),
    )
    row_slot, cot_slot = row_slot.astype(F32), cot_slot.astype(F32)
    left, right = [], []
    for index in range(count):
        own = rank[index : index + 1, :]
        left.append(jnp.where(own == row_slot, 1.0, 0.0))
        right.append(jnp.where(own == cot_slot, weight[index : index + 1, :], 0.0))
    pick = jnp.concatenate([jnp.concatenate(left, 0), jnp.concatenate(right, 0)], 1).astype(BF16)
    return jnp.dot(pick, data, preferred_element_type=F32).astype(BF16)


def own_pack_kernel(caps, ids_ref, probs_ref, share_ref, data_ref, out_ref):
    half, cap_own, cap_rep, tokens = caps
    base = lax.axis_index("expert") // half * half
    out_ref[...] = pack_rows(
        ids_ref[...], probs_ref[...].astype(F32), data_ref[: 2 * tokens, :], share_ref, base, half, half, cap_own, cap_rep
    )


def far_pack_kernel(caps, share_ref, outer_ref, inner_ref, out_ref):
    half, cap_own, cap_rep, tokens, top = caps
    me = lax.axis_index("expert")
    base = me // half * half
    block = me // (half // 2)
    outer = jnp.where((block == 0) | (block == 3), 1, 0)
    data = jnp.where(outer == 1, outer_ref[...], inner_ref[...])
    meta = data[2 * tokens :, :tokens].astype(F32)
    out_ref[...] = pack_rows(
        meta[:top].astype(jnp.int32), meta[top : 2 * top], data[: 2 * tokens, :], share_ref, base, half, half, cap_own, cap_rep
    )


def quotient(value, by):
    return jnp.floor((value.astype(F32) + 0.5) / by)


def expert_rows(cap, recv_ref, gate_ref, up_ref, down_ref):
    main, rest, chunk = slot_plan(cap)
    sources = recv_ref.shape[0]
    width = recv_ref.shape[2]
    inputs = recv_ref[:, :main, :].astype(F32).reshape(sources * main, width).astype(BF16)
    scaled = recv_ref[:, main : 2 * main, :].astype(F32).reshape(sources * main, width).astype(BF16)
    if rest:
        extra = chunk - 2 * main
        mixed = recv_ref[:, 2 * main :, :].astype(F32).reshape(sources * extra, width).astype(BF16)
        shape = (sources * rest, sources * extra)
        row = lax.broadcasted_iota(jnp.int32, shape, 0).astype(F32)
        column = lax.broadcasted_iota(jnp.int32, shape, 1).astype(F32)
        source = quotient(row, rest)
        wanted = source * extra + (row - source * rest)
        pick_rows = jnp.where(column == wanted, 1.0, 0.0).astype(BF16)
        pick_cots = jnp.where(column == wanted + rest, 1.0, 0.0).astype(BF16)
        inputs = jnp.concatenate([inputs, jnp.dot(pick_rows, mixed, preferred_element_type=F32).astype(BF16)], 0)
        scaled = jnp.concatenate([scaled, jnp.dot(pick_cots, mixed, preferred_element_type=F32).astype(BF16)], 0)
    gate_act = jnp.dot(inputs, gate_ref[...], preferred_element_type=F32)
    up_act = jnp.dot(inputs, up_ref[...], preferred_element_type=F32)
    hidden_cot = lax.dot_general(scaled, down_ref[...], (((1,), (1,)), ((), ())), preferred_element_type=F32)
    sigmoid = 1.0 / (1.0 + jnp.exp(-gate_act))
    silu = gate_act * sigmoid
    hidden = (silu * up_act).astype(BF16)
    gate_pre = (hidden_cot * up_act * sigmoid * (1.0 + gate_act * (1.0 - sigmoid))).astype(BF16)
    up_pre = (hidden_cot * silu).astype(BF16)
    dots = jnp.sum(hidden.astype(F32) * hidden_cot, axis=1, keepdims=True)
    total = sources * cap
    row = lax.broadcasted_iota(jnp.int32, (total, 128), 0).astype(F32)
    lane = lax.broadcasted_iota(jnp.int32, (total, 128), 1).astype(F32)
    edge = float(sources * main)
    slot = jnp.where(row < edge, row - quotient(row, main) * main, main + (row - edge) - quotient(row - edge, max(rest, 1)) * rest)
    spread = jnp.where(lane == slot, dots, 0.0)
    row = lax.broadcasted_iota(jnp.int32, (sources, total), 1).astype(F32)
    source = jnp.where(row < edge, quotient(row, main), quotient(row - edge, max(rest, 1)))
    mine = jnp.where(source == lax.broadcasted_iota(jnp.int32, (sources, total), 0).astype(F32), 1.0, 0.0)
    table = jnp.dot(mine, spread, precision=lax.Precision.HIGHEST, preferred_element_type=F32)
    return inputs, scaled, gate_pre, up_pre, hidden, table


def near_kernel(cap, recv_ref, gate_ref, up_ref, down_ref, *out_refs):
    for ref, part in zip(out_refs, expert_rows(cap, recv_ref, gate_ref, up_ref, down_ref)):
        ref[...] = part


def far_kernel(cap, recv_ref, gate_ref, up_ref, down_ref, near_ref, *out_refs):
    half = recv_ref.shape[0]
    quarter = half // 2
    parts = expert_rows(cap, recv_ref, gate_ref, up_ref, down_ref)
    for ref, part in zip(out_refs, parts[:5]):
        ref[...] = part
    table, table_ref = parts[5], out_refs[5]
    base = pl.multiple_of(lax.axis_index("expert") // half * half, 8)
    other = pl.multiple_of(half - base, 8)
    table_ref[pl.ds(base, half), :] = near_ref[...]
    table_ref[pl.ds(other, half), :] = jnp.concatenate([table[quarter:], table[:quarter]], 0)


def grad_kernel(x1, x2, s1, s2, g1, g2, u1, u2, h1, h2, gate_ref, up_ref, down_ref):
    step = pl.program_id(0)
    block = gate_ref.shape[0]
    part = down_ref.shape[1]
    columns = pl.ds(pl.multiple_of(step * block, 128), block)

    def product(left, right):
        return lax.dot_general(left, right, (((0,), (0,)), ((), ())), preferred_element_type=F32)

    x = jnp.concatenate([x1[:, columns], x2[:, columns]], 0)
    gate_ref[...] = product(x, jnp.concatenate([g1[...], g2[...]], 0))
    up_ref[...] = product(x, jnp.concatenate([u1[...], u2[...]], 0))
    columns = pl.ds(pl.multiple_of(step * part, 128), part)
    s = jnp.concatenate([s1[:, columns], s2[:, columns]], 0)
    down_ref[...] = product(jnp.concatenate([h1[...], h2[...]], 0), s)


def finish_kernel(caps, ids_ref, probs_ref, share_ref, table_ref, out_ref):
    half, cap_own, cap_rep = caps
    ids = ids_ref[...]
    table = table_ref[...]
    count = table.shape[0]
    expert, rank = ranks(ids, share_ref, 0, count, half, cap_own, cap_rep)
    found = jnp.zeros(rank.shape, F32)
    for slot in range(cap_own + cap_rep):
        found = found + jnp.where(rank == float(slot), table[:, slot : slot + 1], 0.0)
    lines = []
    for choice in range(ids.shape[0]):
        lines.append(jnp.sum(jnp.where(ids[choice : choice + 1, :] == expert, found, 0.0), axis=0, keepdims=True))
    out_ref[...] = jnp.concatenate(lines, 0) / probs_ref[...].astype(F32)


def call(kernel, outs, in_specs):
    return pl.pallas_call(
        kernel,
        out_shape=outs,
        in_specs=in_specs,
        out_specs=jax.tree.map(lambda _: VMEM, outs),
        compiler_params=pltpu.CompilerParams(vmem_limit_bytes=48 * 1024 * 1024),
    )


def per_device(
    tokens, cotangent, expert_ids, gate_probs, home_share, gate_weight, up_weight, down_weight
):
    experts = lax.axis_size("expert")
    rows, width = tokens.shape
    top = expert_ids.shape[1]
    cap_own = rows * top // experts
    cap_rep = cap_own // 4
    cap = cap_own + cap_rep
    half = experts // 2
    quarter = experts // 4
    hidden_units = gate_weight.shape[2]
    chunk = slot_plan(cap)[2]
    groups = [list(range(half)), list(range(half, experts))]
    mirror = [(e, (3 - e // quarter) * quarter + e % quarter) for e in range(experts)]
    outer = [pair for pair in mirror if pair[0] // quarter in (0, 3)]
    inner = [pair for pair in mirror if pair[0] // quarter in (1, 2)]
    struct = jax.ShapeDtypeStruct

    ids, probs = expert_ids.T, gate_probs.T
    meta = jnp.concatenate([ids.astype(BF16), probs], 0)
    meta = jnp.pad(meta, ((0, -2 * top % 8), (0, width - rows)))
    data = jnp.concatenate([tokens, cotangent, meta], 0)
    far_outer = lax.ppermute(data, "expert", outer)
    near_send = call(
        functools.partial(own_pack_kernel, (half, cap_own, cap_rep, rows)),
        struct((half * chunk, width), BF16),
        [VMEM, VMEM, SMEM, VMEM],
    )(ids, probs, home_share, data)
    near_send, data = lax.optimization_barrier((near_send, data))
    exchange = functools.partial(
        lax.all_to_all, axis_name="expert", split_axis=0, concat_axis=0, axis_index_groups=groups, tiled=True
    )
    near = exchange(near_send.reshape(half, chunk, width))
    far_inner = lax.ppermute(data, "expert", inner)
    far_send = call(
        functools.partial(far_pack_kernel, (half, cap_own, cap_rep, rows, top)),
        struct((half * chunk, width), BF16),
        [SMEM, VMEM, VMEM],
    )(home_share, far_outer, far_inner)
    far = exchange(far_send.reshape(half, chunk, width))

    weights = (gate_weight[0], up_weight[0], down_weight[0])
    total = half * cap
    kept = (
        struct((total, width), BF16),
        struct((total, width), BF16),
        struct((total, hidden_units), BF16),
        struct((total, hidden_units), BF16),
        struct((total, hidden_units), BF16),
    )
    first = call(functools.partial(near_kernel, cap), kept + (struct((half, 128), F32),), [VMEM] * 4)(near, *weights)
    second = call(functools.partial(far_kernel, cap), kept + (struct((experts, 128), F32),), [VMEM] * 5)(
        far, *weights, first[5]
    )
    back = lax.all_to_all(
        second[5].reshape(experts, 1, 128), "expert", split_axis=0, concat_axis=0, tiled=True
    ).reshape(experts, 128)
    steps = 4
    grads = pl.pallas_call(
        grad_kernel,
        grid=(steps,),
        out_shape=(
            struct((width, hidden_units), F32),
            struct((width, hidden_units), F32),
            struct((hidden_units, width), F32),
        ),
        in_specs=[VMEM] * 10,
        out_specs=(
            pl.BlockSpec((width // steps, hidden_units), lambda i: (i, 0)),
            pl.BlockSpec((width // steps, hidden_units), lambda i: (i, 0)),
            pl.BlockSpec((hidden_units, width // steps), lambda i: (0, i)),
        ),
    )(*[part for pair in zip(first[:5], second[:5]) for part in pair])
    gate_cot = call(
        functools.partial(finish_kernel, (half, cap_own, cap_rep)),
        struct((top, rows), F32),
        [VMEM, VMEM, SMEM, VMEM],
    )(ids, probs, home_share, back).T
    if lax.axis_size("dp") > 1:
        grads = tuple(
            lax.psum_scatter(grad.astype(BF16), "dp", scatter_dimension=0, tiled=True).astype(F32) for grad in grads
        )
    return (gate_cot, grads[0][None], grads[1][None], grads[2][None])


def solution(mesh):
    return jax.shard_map(
        per_device,
        mesh=mesh,
        in_specs=(
            P(("dp", "expert"), None),
            P(("dp", "expert"), None),
            P(("dp", "expert"), None),
            P(("dp", "expert"), None),
            P(),
            P("expert", None, None),
            P("expert", None, None),
            P("expert", None, None),
        ),
        out_specs=(
            P(("dp", "expert"), None),
            P("expert", "dp", None),
            P("expert", "dp", None),
            P("expert", "dp", None),
        ),
        check_vma=False,
    )
```

time: 309 us -> 90.5 us (0.29)
  waiting for transfers between devices: 152 us -> 36.6 us
  starting transfers between devices: 96.4 us -> 20 us
  matrix products: 18.5 us -> 0 us
  local copies, waits for them, and re-layouts: 31.8 us -> 15.2 us
  Pallas kernels: 0 us -> 14.8 us
  other arithmetic: 7.84 us -> 2.44 us
    all_to_all x4 -> x3, waiting for transfers between devices: 94.3 us -> 12.4 us  [the longest x1 11.4 us: per_device(): far = exchange(far_send.reshape(half, chunk, width))]
    all_to_all x4 -> x3, starting transfers between devices: 82.4 us -> 13.5 us  [the longest x1 6.45 us: per_device(): near = exchange(near_send.reshape(half, chunk, width))]
    ppermute x6 -> x2, waiting for transfers between devices: 57.7 us -> 24.2 us  [the longest x1 24.2 us: per_device(): far_outer = lax.ppermute(data, 'expert', outer)]
    dot_general x12 -> x0, matrix products: 18.5 us -> none  [the longest x2 4.3 us: expert_side(): lax.dot_general(hidden, scaled, (((0,), (0,)), ((), ())), preferred_eleme...]
    pallas_call x0 -> x6, Pallas kernels: none -> 14.8 us  [the longest x1 6.18 us: per_device(): pl.pallas_call(grad_kernel, grid=(steps,), out_shape=(struct((width, hidd...]
    unnamed x28 -> x44, local copies, waits for them, and re-layouts: 3.82 us -> 15.2 us
    scatter x3 -> x0, local copies, waits for them, and re-layouts: 10.2 us -> none  [the longest x1 3.77 us: per_device(): jnp.zeros((slots_total + 1,), jnp.bfloat16).at[position].set(gate_probs)]
    ppermute x6 -> x2, starting transfers between devices: 14 us -> 6.55 us  [the longest x1 5.85 us: per_device(): far_outer = lax.ppermute(data, 'expert', outer)]
  transfers between devices with their start and end apart: 10 -> 5, of which waited for: 8 -> 3; matrix products, arithmetic and copies ran while one was open for 12% -> 0% of each run, Pallas kernels for 0% -> 10%
where the time goes in v1:
time: 90.5 us; the launch traced here: 89.9 us
  waiting for transfers between devices  36.6 us (40%)
  starting transfers between devices  20 us (22%)
  local copies, waits for them, and re-layouts  15.2 us (17%)
  Pallas kernels  14.8 us (16%)
  other arithmetic  2.44 us (3%)
    ppermute x1, waiting for transfers between devices, per_device(): far_outer = lax.ppermute(data, 'expert', outer)  24.2 us
    unnamed x44, local copies, waits for them, and re-layouts  15.2 us
    all_to_all x1, waiting for transfers between devices, per_device(): far = exchange(far_send.reshape(half, chunk, width))  11.4 us
    all_to_all x1, starting transfers between devices, per_device(): near = exchange(near_send.reshape(half, chunk, width))  6.45 us
    pallas_call x1, Pallas kernels, per_device(): pl.pallas_call(grad_kernel, grid=(steps,), out_shape=(struct((width, hidd...  6.18 us
    ppermute x1, starting transfers between devices, per_device(): far_outer = lax.ppermute(data, 'expert', outer)  5.85 us
    all_to_all x1, starting transfers between devices, per_device(): far = exchange(far_send.reshape(half, chunk, width))  4.17 us
    all_to_all x1, starting transfers between devices, per_device(): lax.all_to_all(second[5].reshape(experts, 1, 128), 'expert', split_axis=0...  2.85 us
  transfers between devices with their start and end apart: 5, of which 3 were waited for; matrix products, arithmetic and copies ran while one was open for 0% of the time, Pallas kernels for 10%

profile of v1, /device:TPU:0, one launch (start us, length us, event | category | flops | bytes accessed | tf_op | source)
XLA Modules:
  0.0 89.9 jit_solution(10460453061962494133)
XLA Ops:
  0.6 0.7 bitcast_convert_fusion
  1.3 0.7 fusion.2
  2.0 1.1 %pad_maximum_fusion.data_ref = bf16[264,1024]{1,0:T(8,128)(2,1)S(1)} fusion(bf16[8,1024]{1,0:T(8,128)(2,1)S(1)} %fusion.2, bf16[128,1024]{1,0:T(8,128)(2,1)} %param.9, bf16[128,1024]{1,0:T(8,128)(2,1)} %param.8), kind=kLoop, calls=%fused_computation | loop fusion | flops 1622016 | bytes 1081344 | tf_op jit(solution)/shard_map/concatenate | solution.py:212
  3.1 0.0 copy-start.16
  3.1 0.7 copy-done.16
  3.8 0.0 copy-start.18
  3.8 0.7 copy-done.18
  4.4 0.0 copy-start.20
  4.4 0.7 copy-done.20
  5.1 2.2 %shard_map.111 = bf16[640,1024]{1,0:T(8,128)(2,1)} custom-call(s32[4,128]{1,0:T(4,128)S(1)} %bitcast.24, bf16[4,128]{1,0:T(4,128)(2,1)S(1)} %bitcast.27, s32[16]{0:T(128)S(1)} %copy-done.20, bf16[264,1024]{1,0:T(8,128)(2,1)S(1)} %pad_maximum_fusion.data_ref), custom_call_target="tpu_custom_call" | custom-call | tf_op jit(solution)/shard_map/pallas_call | solution.py:214
  7.3 0.0 copy-start.21
  7.3 6.4 %all-to-all-start.1 = ((bf16[16,40,1024]{2,1,0:T(8,128)(2,1)}), bf16[16,40,1024]{2,1,0:T(8,128)(2,1)S(1)}, u32[]{:S(2)}, u32[]{:S(2)}) async-start(bf16[16,40,1024]{2,1,0:T(8,128)(2,1)} %bitcast.6), calls=%async_computation.1 | async-start | bytes 2621440 | tf_op jit(solution)/shard_map/all_to_all | solution.py:223
  13.8 5.9 %collective-permute-start = (bf16[264,1024]{1,0:T(8,128)(2,1)S(1)}, bf16[264,1024]{1,0:T(8,128)(2,1)S(1)}, u32[]{:S(2)}, u32[]{:S(2)}) collective-permute-start(bf16[264,1024]{1,0:T(8,128)(2,1)S(1)} %pad_maximum_fusion.data_ref), channel_id=1, source_target_pairs={{0,24},{1,25},{2,26},{3,27},{4,28},{5,29},{6,30},{7,31},{24,0},{25... | collective-permute-start | bytes 1622024 | tf_op jit(solution)/shard_map/ppermute | solution.py:213
  19.6 0.7 collective-permute-start.1
  20.3 24.2 %collective-permute-done.outer_ref = bf16[264,1024]{1,0:T(8,128)(2,1)S(1)} collective-permute-done((bf16[264,1024]{1,0:T(8,128)(2,1)S(1)}, bf16[264,1024]{1,0:T(8,128)(2,1)S(1)}, u32[]{:S(2)}, u32[]{:S(2)}) %collective-permute-start) | collective-permute-done | bytes 540704 | tf_op jit(solution)/shard_map/ppermute | solution.py:213
  44.5 0.0 collective-permute-done.1.inner_ref
  44.5 0.0 copy-done.21
  44.5 1.2 %shard_map.112 = bf16[640,1024]{1,0:T(8,128)(2,1)S(1)} custom-call(s32[16]{0:T(128)S(1)} %copy-done.21, bf16[264,1024]{1,0:T(8,128)(2,1)S(1)} %collective-permute-done.outer_ref, bf16[264,1024]{1,0:T(8,128)(2,1)S(1)} %collective-permute-done.1.inner_ref), custom_call_target="tpu_custom_call" | custom-call | tf_op jit(solution)/shard_map/pallas_call | solution.py:225
  45.7 0.0 copy-start
  45.8 1.0 %copy-done = bf16[640,1024]{1,0:T(8,128)(2,1)} copy-done((bf16[640,1024]{1,0:T(8,128)(2,1)}, bf16[640,1024]{1,0:T(8,128)(2,1)S(1)}, u32[]{:S(2)}) %copy-start) | copy-done | bytes 1310744
  46.8 0.0 all-to-all-done.1.recv_ref
  46.8 0.0 copy-start.1
  46.8 4.2 %all-to-all-start = ((bf16[16,40,1024]{2,1,0:T(8,128)(2,1)}), bf16[16,40,1024]{2,1,0:T(8,128)(2,1)S(1)}, u32[]{:S(2)}, u32[]{:S(2)}) async-start(bf16[16,40,1024]{2,1,0:T(8,128)(2,1)} %bitcast.16), calls=%async_computation | async-start | bytes 2621440 | tf_op jit(solution)/shard_map/all_to_all | solution.py:230
  51.0 0.0 copy-done.1
  51.0 0.0 copy-start.2
  51.0 1.1 %copy-done.2 = bf16[1,1024,384]{2,1,0:T(8,128)(2,1)S(1)} copy-done((bf16[1,1024,384]{2,1,0:T(8,128)(2,1)S(1)}, bf16[1,1024,384]{2,1,0:T(8,128)(2,1)}, u32[]{:S(2)}) %copy-start.2) | copy-done | bytes 786456
  52.1 0.0 copy-start.4
  52.1 1.1 %copy-done.4 = bf16[1,384,1024]{2,1,0:T(8,128)(2,1)S(1)} copy-done((bf16[1,384,1024]{2,1,0:T(8,128)(2,1)S(1)}, bf16[1,384,1024]{2,1,0:T(8,128)(2,1)}, u32[]{:S(2)}) %copy-start.4) | copy-done | bytes 786456
  53.3 1.6 %shard_map.113 = (bf16[320,1024]{1,0:T(8,128)(2,1)S(1)}, bf16[320,1024]{1,0:T(8,128)(2,1)S(1)}, bf16[320,384]{1,0:T(8,128)(2,1)S(1)}, bf16[320,384]{1,0:T(8,128)...) custom-call(bf16[16,40,1024]{2,1,0:T(8,128)(2,1)S(1)} %all-to-all-done.1.recv_ref, ...), custom_call_target="tpu_custom_call" | custom-call | tf_op jit(solution)/shard_map/pallas_call | solution.py:241
  54.9 0.0 copy-start.6
  54.9 0.9 copy-done.6
  55.8 0.0 copy-start.7
  55.8 0.9 copy-done.7
  56.6 0.0 copy-start.10
  56.6 0.7 copy-done.10
  57.4 0.0 copy-start.11
  57.4 0.7 copy-done.11
  58.1 0.0 copy-start.12
  58.1 0.7 copy-done.12
  58.8 11.4 %all-to-all-done.recv_ref = bf16[16,40,1024]{2,1,0:T(8,128)(2,1)S(1)} async-done(((bf16[16,40,1024]{2,1,0:T(8,128)(2,1)}), bf16[16,40,1024]{2,1,0:T(8,128)(2,1)S(1)}, u32[]{:S(2)}, u32[]{:S(2)}) %all-to-all-start) | async-done | bytes 1310752 | tf_op jit(solution)/shard_map/all_to_all | solution.py:230
  70.2 0.0 copy-start.3
  70.2 1.1 %copy-done.3 = bf16[1,1024,384]{2,1,0:T(8,128)(2,1)S(1)} copy-done((bf16[1,1024,384]{2,1,0:T(8,128)(2,1)S(1)}, bf16[1,1024,384]{2,1,0:T(8,128)(2,1)}, u32[]{:S(2)}) %copy-start.3) | copy-done | bytes 786456
  71.3 0.0 copy-start.5
  71.3 1.1 %copy-done.5 = bf16[1,384,1024]{2,1,0:T(8,128)(2,1)S(1)} copy-done((bf16[1,384,1024]{2,1,0:T(8,128)(2,1)S(1)}, bf16[1,384,1024]{2,1,0:T(8,128)(2,1)}, u32[]{:S(2)}) %copy-start.5) | copy-done | bytes 786456
  72.5 2.3 %shard_map.114 = (bf16[320,1024]{1,0:T(8,128)(2,1)S(1)}, bf16[320,1024]{1,0:T(8,128)(2,1)S(1)}, bf16[320,384]{1,0:T(8,128)(2,1)S(1)}, bf16[320,384]{1,0:T(8,128)...) custom-call(bf16[16,40,1024]{2,1,0:T(8,128)(2,1)S(1)} %all-to-all-done.recv_ref, ...), custom_call_target="tpu_custom_call" | custom-call | tf_op jit(solution)/shard_map/pallas_call | solution.py:242
  74.7 0.0 copy-start.8
  74.7 0.8 copy-done.8
  75.6 0.0 copy-start.9
  75.6 0.9 copy-done.9
  76.4 0.0 copy-start.13
  76.4 0.7 copy-done.13
  77.1 0.0 copy-start.14
  77.1 0.7 copy-done.14
  77.8 0.0 copy-start.15
  77.8 0.7 copy-done.15
  78.5 2.9 %all-to-all-start.2 = ((f32[32,1,128]{2,1,0:T(1,128)}), f32[32,1,128]{2,1,0:T(1,128)S(1)}, u32[]{:S(2)}, u32[]{:S(2)}) async-start(f32[32,1,128]{2,1,0:T(1,128)} %bitcast.8), calls=%async_computation.2 | async-start | bytes 32768 | tf_op jit(solution)/shard_map/all_to_all | solution.py:245
  81.4 0.0 copy-start.17
  81.4 0.0 copy-start.19
  81.4 6.2 %shard_map.116 = (f32[1024,384]{1,0:T(8,128)}, f32[1024,384]{1,0:T(8,128)}, f32[384,1024]{1,0:T(8,128)}) custom-call(bf16[320,1024]{1,0:T(8,128)(2,1)} %copy-done.6, bf16[320,1024]{1,0:T(8,128)(2,1)} %copy-done.8, bf16[320,1024]{1,0:T(8,128)(2,1)} %copy-done.7, bf16[320,1024]{1,0:T(8,128)(2,1)} %copy-done.9, bf16[320,384]{1,0:T(8,128)(2,1)} %copy-done.10, ...), custom_call_target="tpu_custom_call" | custom-call | tf_op jit(solution)/shard_map/pallas_call | solution.py:249
  87.6 1.0 %all-to-all-done.2 = f32[32,1,128]{2,1,0:T(1,128)S(1)} async-done(((f32[32,1,128]{2,1,0:T(1,128)}), f32[32,1,128]{2,1,0:T(1,128)S(1)}, u32[]{:S(2)}, u32[]{:S(2)}) %all-to-all-start.2) | async-done | bytes 16416 | tf_op jit(solution)/shard_map/all_to_all | solution.py:245
  88.5 0.0 copy-done.17
  88.5 0.0 copy-done.19
  88.6 1.3 %shard_map.115 = f32[4,128]{1,0:T(4,128)} custom-call(s32[4,128]{1,0:T(4,128)S(1)} %bitcast.25, bf16[4,128]{1,0:T(4,128)(2,1)S(1)} %bitcast.28, s32[16]{0:T(128)S(1)} %copy-done.21, f32[32,128]{1,0:T(8,128)S(1)} %bitcast.23), custom_call_target="tpu_custom_call" | custom-call | tf_op jit(solution)/shard_map/pallas_call | solution.py:264
Async XLA Ops:
  3.1 0.7 copy-start.16
  3.8 0.7 copy-start.18
  4.4 0.7 copy-start.20
  7.3 37.2 %copy-start.21 = (s32[16]{0:T(128)S(1)}, s32[16]{0:T(128)}, u32[]{:S(2)}) copy-start(s32[16]{0:T(128)} %share_ref.5) | copy-start | bytes 196
  7.3 39.5 %all-to-all-start.1 = ((bf16[16,40,1024]{2,1,0:T(8,128)(2,1)}), bf16[16,40,1024]{2,1,0:T(8,128)(2,1)S(1)}, u32[]{:S(2)}, u32[]{:S(2)}) async-start(bf16[16,40,1024]{2,1,0:T(8,128)(2,1)} %bitcast.6), calls=%async_computation.1 | async-start | bytes 2621440 | tf_op jit(solution)/shard_map/all_to_all | solution.py:223
  13.8 30.8 %collective-permute-start = (bf16[264,1024]{1,0:T(8,128)(2,1)S(1)}, bf16[264,1024]{1,0:T(8,128)(2,1)S(1)}, u32[]{:S(2)}, u32[]{:S(2)}) collective-permute-start(bf16[264,1024]{1,0:T(8,128)(2,1)S(1)} %pad_maximum_fusion.data_ref), channel_id=1, source_target_pairs={{0,24},{1,25},{2,26},{3,27},{4,28},{5,29},{6,30},{7,31},{24,0},{25... | collective-permute-start | bytes 1622024 | tf_op jit(solution)/shard_map/ppermute | solution.py:213
  19.6 24.9 %collective-permute-start.1 = (bf16[264,1024]{1,0:T(8,128)(2,1)S(1)}, bf16[264,1024]{1,0:T(8,128)(2,1)S(1)}, u32[]{:S(2)}, u32[]{:S(2)}) collective-permute-start(bf16[264,1024]{1,0:T(8,128)(2,1)S(1)} %pad_maximum_fusion.data_ref), channel_id=1, source_target_pairs={{8,16},{9,17},{10,18},{11,19},{12,20},{13,21},{14,22},{15,23},{16,... | collective-permute-start | bytes 1622024 | tf_op jit(solution)/shard_map/ppermute | solution.py:224
  45.7 1.1 %copy-start = (bf16[640,1024]{1,0:T(8,128)(2,1)}, bf16[640,1024]{1,0:T(8,128)(2,1)S(1)}, u32[]{:S(2)}) copy-start(bf16[640,1024]{1,0:T(8,128)(2,1)S(1)} %shard_map.112) | copy-start | bytes 3932164
  46.8 4.2 %copy-start.1 = (bf16[1,1024,384]{2,1,0:T(8,128)(2,1)S(1)}, bf16[1,1024,384]{2,1,0:T(8,128)(2,1)}, u32[]{:S(2)}) copy-start(bf16[1,1024,384]{2,1,0:T(8,128)(2,1)} %param.13) | copy-start | bytes 2359300
  46.8 23.4 %all-to-all-start = ((bf16[16,40,1024]{2,1,0:T(8,128)(2,1)}), bf16[16,40,1024]{2,1,0:T(8,128)(2,1)S(1)}, u32[]{:S(2)}, u32[]{:S(2)}) async-start(bf16[16,40,1024]{2,1,0:T(8,128)(2,1)} %bitcast.16), calls=%async_computation | async-start | bytes 2621440 | tf_op jit(solution)/shard_map/all_to_all | solution.py:230
  51.0 1.1 %copy-start.2 = (bf16[1,1024,384]{2,1,0:T(8,128)(2,1)S(1)}, bf16[1,1024,384]{2,1,0:T(8,128)(2,1)}, u32[]{:S(2)}) copy-start(bf16[1,1024,384]{2,1,0:T(8,128)(2,1)} %param.14) | copy-start | bytes 2359300
  52.1 1.1 %copy-start.4 = (bf16[1,384,1024]{2,1,0:T(8,128)(2,1)S(1)}, bf16[1,384,1024]{2,1,0:T(8,128)(2,1)}, u32[]{:S(2)}) copy-start(bf16[1,384,1024]{2,1,0:T(8,128)(2,1)} %param.15) | copy-start | bytes 2359300
  54.9 0.9 copy-start.6
  55.8 0.9 copy-start.7
  56.6 0.7 copy-start.10
  57.4 0.7 copy-start.11
  58.1 0.7 copy-start.12
  70.2 1.1 %copy-start.3 = (bf16[1,1024,384]{2,1,0:T(8,128)(2,1)S(1)}, bf16[1,1024,384]{2,1,0:T(8,128)(2,1)}, u32[]{:S(2)}) copy-start(bf16[1,1024,384]{2,1,0:T(8,128)(2,1)} %param.14) | copy-start | bytes 2359300
  71.3 1.1 %copy-start.5 = (bf16[1,384,1024]{2,1,0:T(8,128)(2,1)S(1)}, bf16[1,384,1024]{2,1,0:T(8,128)(2,1)}, u32[]{:S(2)}) copy-start(bf16[1,384,1024]{2,1,0:T(8,128)(2,1)} %param.15) | copy-start | bytes 2359300
  74.7 0.8 copy-start.8
  75.6 0.9 copy-start.9
  76.4 0.7 copy-start.13
  77.1 0.7 copy-start.14
  77.8 0.7 copy-start.15
  78.5 10.0 %all-to-all-start.2 = ((f32[32,1,128]{2,1,0:T(1,128)}), f32[32,1,128]{2,1,0:T(1,128)S(1)}, u32[]{:S(2)}, u32[]{:S(2)}) async-start(f32[32,1,128]{2,1,0:T(1,128)} %bitcast.8), calls=%async_computation.2 | async-start | bytes 32768 | tf_op jit(solution)/shard_map/all_to_all | solution.py:245
  81.4 7.2 %copy-start.17 = (s32[128,4]{0,1:T(4,128)S(1)}, s32[128,4]{0,1:T(4,128)}, u32[]{:S(2)}) copy-start(s32[128,4]{0,1:T(4,128)} %param.10) | copy-start | bytes 6148
  81.4 7.2 %copy-start.19 = (bf16[128,4]{0,1:T(4,128)(2,1)S(1)}, bf16[128,4]{0,1:T(4,128)(2,1)}, u32[]{:S(2)}) copy-start(bf16[128,4]{0,1:T(4,128)(2,1)} %param.11) | copy-start | bytes 3076
